TPU v7x, 256 devices: a whole 4x4x8 slice. The times are simulated.
256 devices in a mesh: rows: 64 (over y, z, core), cols: 4 (over x).
Axes of the slice: x: 4, y: 4, z: 8, core: 2. Of those that a mesh axis runs over, the one named last changes fastest.
Arguments:
- panel: float32 [131072, 256], P(('rows', 'cols')), may hold values from -17 to 17, as said below
- trailing: float32 [131072, 2048], P('rows', 'cols'), may hold values from -6 to 6
Outputs:
- rfactor: float32 [256, 256], replicated
- projected: float32 [256, 2048], P(None, 'cols')
- updated: float32 [131072, 2048], P('rows', 'cols')
Inputs may be any that keep to these rules, and one draw needn't show every extreme that they name: The panel has full column rank with a moderate condition number (under 100); each column has its own scale and a part shared by all columns.
All inputs are finite; a program needn't handle non-finite values.
Results may differ from a plain program's by a relative error of at most 0.000078.
Values sent between devices are 32-bit elements; how exact they have to be, the bound alone decides.
A program may use at most 64 MiB of HBM per device.

v0:
```python
import jax
import jax.numpy as jnp
from jax import lax
from jax.sharding import PartitionSpec as P


def joined_along(tiles, dim):
    tiles = jnp.moveaxis(tiles, 0, dim)
    shape = tiles.shape
    return tiles.reshape(*shape[:dim], shape[dim] * shape[dim + 1], *shape[dim + 2 :])


def copy_for_each(array, axis):
    copies = jnp.broadcast_to(array, (lax.axis_size(axis), *array.shape))
    return lax.all_to_all(copies, axis, split_axis=0, concat_axis=0, tiled=True)


def gather_directly(array, axis, dim):
    return joined_along(copy_for_each(array, axis), dim)


def in_one(arrays, axis):
    ends = [0]
    for a in arrays:
        ends.append(ends[-1] + a.size)
    running = lax.psum(jnp.concatenate([a.ravel() for a in arrays]), axis)
    return tuple((running[b:e].reshape(a.shape) for a, b, e in zip(arrays, ends, ends[1:])))


def inner(left, right):
    return lax.dot_general(
        left,
        right,
        (((0,), (0,)), ((), ())),
        precision=lax.Precision.HIGHEST,
        preferred_element_type=jnp.float32,
    )


def times(left, right):
    return jnp.dot(left, right, precision=lax.Precision.HIGHEST, preferred_element_type=jnp.float32)


def lower_solve(rfactor, right):
    return jax.scipy.linalg.solve_triangular(rfactor.T, right, lower=True)


def shards(panel, trailing):
    block = gather_directly(panel, "cols", 0)
    gram, cross = in_one((inner(block, block), inner(block, trailing)), "rows")
    rfactor = jnp.linalg.cholesky(gram).T
    basis = lower_solve(rfactor, block.T).T
    projected = lower_solve(rfactor, cross)
    updated = trailing - times(basis, projected)
    return (rfactor, projected, updated)


def solution(mesh):
    placed = (P(("rows", "cols"), None), P("rows", "cols"))
    return jax.shard_map(
        shards,
        mesh=mesh,
        in_specs=placed,
        out_specs=(P(), P(None, "cols"), P("rows", "cols")),
        check_vma=False,
    )
```

profile of v0, /device:TPU:1, one launch (start us, length us, event | category | flops | bytes accessed | tf_op | source)
XLA Modules:
  0.0 313.1 jit_solution(15103172928544927577)
XLA Ops:
  7.2 1.2 broadcast_in_dim.5
  8.4 30.0 %all_to_all.5 = f32[4,512,256]{2,1,0:T(8,128)S(1)} all-to-all(f32[4,512,256]{2,1,0:T(8,128)S(1)} %broadcast_in_dim.5), channel_id=1, replica_groups=mesh['rows'=64,'cols'=4] {'cols'}, dimensions={0} | all-to-all | bytes 4194304 | tf_op jit(solution)/shard_map/all_to_all | solution.py:15
  38.4 3.5 %convolution_bitcast_fusion.1 = f32[32,2,8,128]{3,2,1,0:T(8,128)S(1)} fusion(f32[4,512,256]{2,1,0:T(8,128)S(1)} %all_to_all.5), kind=kOutput, calls=%fused_computation.9 | convolution fusion | flops 1610612736 | bytes 2359296 | tf_op jit(solution)/shard_map/dot_general | solution.py:31
  42.1 3.7 %convolution_bitcast_fusion = f32[32,4,8,128]{3,2,1,0:T(8,128)S(1)} fusion(f32[2048,256]{1,0:T(8,128)S(1)} %bitcast.53, f32[2048,512]{1,0:T(8,128)S(1)} %copy-done), kind=kOutput, calls=%fused_computation.7 | convolution fusion | flops 3221225472 | bytes 6815744 | tf_op jit(solution)/shard_map/dot_general | solution.py:31
  45.9 0.9 pad_maximum_fusion
  46.9 186.6 %all-reduce.3.cloned.1.call-done = f32[196608]{0:T(1024)} async-done(((f32[196608]{0:T(1024)}), f32[196608]{0:T(1024)}) %all-reduce.3.cloned.1.call-update) | async-done | bytes 786448 | tf_op jit(solution)/shard_map/psum | solution.py:26
  233.4 1.2 fusion.18
  234.9 11.7 %cholesky.50 = f32[128,128]{1,0:T(8,128)S(1)} custom-call(f32[128,128]{1,0:T(8,128)S(1)} %cholesky.118), custom_call_target="Cholesky" | custom-call | tf_op jit(solution)/shard_map/jit(cholesky)/cholesky | solution.py:51
  246.7 9.9 %custom-call.18 = f32[1,128,128]{1,2,0:T(8,128)S(1)} custom-call(f32[1,128,128]{2,1,0:T(8,128)S(1)} %get-tuple-element.35), custom_call_target="InvertDiagBlocksLowerTriangular" | custom-call | tf_op jit(solution)/shard_map/jit(cholesky)/cholesky | solution.py:51
  257.1 11.7 %cholesky.105 = f32[128,128]{1,0:T(8,128)S(1)} custom-call(f32[128,128]{1,0:T(8,128)S(1)} %convolution_subtract_fusion.3), custom_call_target="Cholesky" | custom-call | tf_op jit(solution)/shard_map/jit(cholesky)/cholesky | solution.py:51
  268.9 0.6 compare_reduce_fusion
  270.8 0.8 copy.10
  271.7 4.0 %while.1 = (s32[]{:T(128)}, f32[256,256]{1,0:T(8,128)S(1)}, s32[2,2]{1,0:T(2,128)S(1)}, f32[2,128,128]{2,1,0:T(8,128)S(1)}, s32[]{:T(128)}) while((s32[]{:T(128)}, f32[256,256]{1,0:T(8,128)S(1)}, s32[2,2]{1,0:T(2,128)S(1)}, f32[2,128,128]{2,1,0:T(8,128)S(1)}, s32[]{:T(128)}) %tuple.32), condition=%wide.while_cond, body=%wide.while_body.sunk | while | flops 2 | bytes 131189 | solution.py:45
  271.8 0.6 fusion.32
  272.3 1.4 bitcast_dynamic-update-slice_fusion.2
  273.8 0.6 fusion.32
  274.3 1.4 bitcast_dynamic-update-slice_fusion.2
  275.7 19.9 %custom-call.19 = f32[2,128,128]{1,2,0:T(8,128)S(1)} custom-call(f32[2,128,128]{2,1,0:T(8,128)S(1)} %get-tuple-element.10), custom_call_target="InvertDiagBlocksLowerTriangular" | custom-call | tf_op jit(solution)/shard_map/jit(_solve_triangular)/triangular_solve | solution.py:45
  295.7 0.4 fusion.11
  296.5 0.4 fusion.13
  297.0 1.1 fusion.3
  298.1 1.8 convolution_subtract_fusion.1
  299.9 1.1 fusion.12
  301.0 5.2 %convolution_subtract_fusion = f32[2048,512]{1,0:T(8,128)} fusion(f32[2048,512]{1,0:T(8,128)S(1)} %copy-done.1, f32[256,512]{1,0:T(8,128)S(1)} %pad_maximum_fusion.1, f32[128,2048]{1,0:T(8,128)S(1)} %fusion.12, f32[128,2048]{1,0:T(8,128)S(1)} %fusion.3), kind=kOutput, calls=%fused_computation.2 | convolution fusion | flops 3222798336 | bytes 11010048 | tf_op jit(solution)/shard_map/dot_general | solution.py:41
  (29 shorter events, 1.8 us)
Async XLA Ops:
  7.2 226.3 %all-reduce.3.cloned.1.call-start = ((), (), s32[]{:S(2)}) async-start(), calls=%async_computation.1 | async-start | bytes 1572864 | tf_op jit(solution)/shard_map/psum | solution.py:26
  38.4 3.6 %copy-start = (f32[2048,512]{1,0:T(8,128)S(1)}, f32[2048,512]{1,0:T(8,128)}, u32[]{:S(2)}) copy-start(f32[2048,512]{1,0:T(8,128)} %param.3) | copy-start | bytes 12582916
  297.0 4.0 %copy-start.2 = (f32[256,512]{1,0:T(8,128)}, f32[256,512]{1,0:T(8,128)S(1)}, u32[]{:S(2)}) copy-start(f32[256,512]{1,0:T(8,128)S(1)} %pad_maximum_fusion.1) | copy-start | bytes 1572868
  298.1 2.9 copy-start.1
Sparse Core Ops, SparseCore 0:
  47.0 186.4 all-reduce.2
where the time goes:
time: 314 us; the launch traced here: 313 us
  waiting for transfers between devices  187 us (60%)
  other arithmetic  55 us (18%)
  blocking collectives  30 us (10%)
  matrix products  18 us (6%)
  between operations  15.6 us (5%)
  local copies, waits for them, and re-layouts  7.82 us (2%)
    psum x1, waiting for transfers between devices, in_one(): running = lax.psum(jnp.concatenate([a.ravel() for a in arrays]), axis)  187 us
    another operation x6, other arithmetic, shards(): rfactor = jnp.linalg.cholesky(gram).T  34.1 us
    all_to_all x1, blocking collectives, copy_for_each(): return lax.all_to_all(copies, axis, split_axis=0, concat_axis=0, tiled=True)  30 us
    another operation x4, other arithmetic, lower_solve(): return jax.scipy.linalg.solve_triangular(rfactor.T, right, lower=True)  20 us
    dot_general x2, matrix products, inner(): lax.dot_general(left, right, (((0,), (0,)), ((), ())), precision=lax.Prec...  7.15 us
  transfers between devices with their start and end apart: 1, of which 1 were waited for; matrix products, arithmetic and copies ran while one was open for 0% of the time, Pallas kernels for 0%

commit v1 on v0

v1 whole, which is shorter than its diff:
```python
import functools

import jax
import jax.numpy as jnp
from jax import lax
from jax.experimental import pallas as pl
from jax.experimental.pallas import tpu as pltpu
from jax.sharding import PartitionSpec as P

MESH = pl.DeviceIdType.MESH
HIGHEST = lax.Precision.HIGHEST
F32 = jnp.float32


def dot(left, right):
    return jnp.dot(left, right, precision=HIGHEST, preferred_element_type=F32)


class Place:
    def __init__(self):
        rows = lax.axis_index("rows")
        self.x = lax.axis_index("cols")
        self.core = lax.rem(rows, 2)
        self.z = lax.rem(rows // 2, 8)
        self.y = rows // 16

    def at(self, y=0, z=0, core=0, x=0):
        there = lax.rem(self.y + y, 4) * 16 + lax.rem(self.z + z, 8) * 2 + lax.rem(self.core + core, 2)
        return (there, lax.rem(self.x + x, 4))


def send(src, dst, send_sem, recv_sem, device):
    copy = pltpu.make_async_remote_copy(
        src_ref=src, dst_ref=dst, send_sem=send_sem, recv_sem=recv_sem, device_id=device, device_id_type=MESH
    )
    copy.start()
    return copy


class Reduction:
    def __init__(self, place, refs, over_x):
        self.place, self.over_x = place, over_x
        self.part, self.from_core, self.s1, self.from_y, self.s2, self.from_z, self.s3, self.from_x, self.full = refs[:9]
        self.send_sem, self.recv_sem = refs[9:]
        self.copies = []
        self.used = 0

    def send(self, src, dst, device):
        copy = send(src, dst, self.send_sem.at[self.used], self.recv_sem.at[self.used], device)
        self.used += 1
        self.copies.append(copy)
        return copy

    def start_core(self):
        p = self.place
        self.c1 = self.send(self.part.at[pl.ds(16 * (1 - p.core), 16)], self.from_core, p.at(core=1))

    def start_y(self):
        p = self.place
        self.c1.wait_recv()
        self.s1[...] = self.part[pl.ds(16 * p.core, 16)] + self.from_core[...]
        self.c2 = [
            self.send(self.s1.at[pl.ds(4 * lax.rem(p.y + d, 4), 4)], self.from_y.at[d - 1], p.at(y=d)) for d in (2, 1, 3)
        ]

    def start_z(self):
        p = self.place
        for c in self.c2:
            c.wait_recv()
        self.s2[...] = (self.s1[pl.ds(4 * p.y, 4)] + self.from_y[0]) + (self.from_y[1] + self.from_y[2])
        self.c3 = []
        for d in (4, 3, 5, 2, 6, 1, 7):
            there = lax.rem(p.z + d, 8)
            self.c3.append(self.send(self.s2.at[there // 2, lax.rem(there, 2)], self.from_z.at[d - 1], p.at(z=d)))

    def end_z(self):
        p = self.place
        for c in self.c3:
            c.wait_recv()
        total = self.s2[p.z // 2, lax.rem(p.z, 2)]
        for d in range(7):
            total = total + self.from_z[d]
        return total

    def start_x(self):
        p = self.place
        self.s3[...] = self.end_z()
        self.c4 = [self.send(self.s3, self.from_x.at[p.x], p.at(x=d)) for d in (2, 1, 3)]
        self.from_x[p.x] = self.s3[...]

    def start_gather_z(self):
        p = self.place
        group, half = 16 * p.core + 4 * p.y + p.z // 2, lax.rem(p.z, 2)
        if self.over_x:
            for c in self.c4:
                c.wait_recv()
            self.full[group, half] = (self.from_x[0] + self.from_x[1]) + (self.from_x[2] + self.from_x[3])
        else:
            self.full[group, half] = self.end_z()
        mine = self.full.at[group, half]
        self.c5 = [self.send(mine, mine, p.at(z=d)) for d in (4, 3, 5, 2, 6, 1, 7)]

    def start_gather_y(self):
        p = self.place
        for c in self.c5:
            c.wait_recv()
        mine = self.full.at[pl.ds(16 * p.core + 4 * p.y, 4)]
        self.c6 = [self.send(mine, mine, p.at(y=d)) for d in (2, 1, 3)]
        self.c7 = [self.send(mine, mine, p.at(core=1))]

    def start_gather_core(self):
        p = self.place
        for c, d in zip(self.c6, (2, 1, 3)):
            c.wait_recv()
            theirs = self.full.at[pl.ds(16 * p.core + 4 * lax.rem(p.y + 4 - d, 4), 4)]
            self.c7.append(self.send(theirs, theirs, p.at(core=1)))

    def finish(self):
        for c in self.c7:
            c.wait_recv()

    def drain(self):
        for c in self.copies:
            c.wait_send()


def halves(ref, width):
    return jnp.concatenate([ref[:, h].reshape(256, width // 2) for h in range(2)], axis=1)


def reduce_kernel(panel, trailing, block, gram, cross, held, load_sem, side_send, side_recv, *rest):
    p = Place()
    g = Reduction(p, (*rest[:8], gram, *rest[8:10]), True)
    t = Reduction(p, (*rest[10:18], cross, *rest[18:20]), False)

    own = pltpu.make_async_copy(panel, block.at[p.x], load_sem.at[0])
    own.start()
    load = pltpu.make_async_copy(trailing, held, load_sem.at[1])
    load.start()

    barrier = pltpu.get_barrier_semaphore()
    peers = [p.at(core=1)] + [p.at(y=d) for d in (1, 2, 3)] + [p.at(z=d) for d in range(1, 8)] + [p.at(x=d) for d in (1, 2, 3)]
    for peer in peers:
        pl.semaphore_signal(barrier, inc=1, device_id=peer, device_id_type=MESH)
    pl.semaphore_wait(barrier, len(peers))

    own.wait()
    steps = (1, 3)
    direct = [[None, None], [None, None]]
    for n in range(2):
        for side in range(2):
            half = n if side == 0 else 1 - n
            rows = block.at[p.x, pl.ds(256 * half, 256)]
            at = 2 * side + half
            direct[side][half] = send(rows, rows, side_send.at[at], side_recv.at[at], p.at(x=steps[side]))

    mine = block[p.x]
    product = dot(mine.T, mine)
    for h in range(2):
        g.part[:, h] = product[:, 128 * h : 128 * h + 128].reshape(32, 8, 128)
    g.start_core()

    load.wait()

    def add_cross(x, first):
        product = dot(block[x].T, held[pl.ds(512 * x, 512), :])
        for h in range(2):
            term = product[:, 256 * h : 256 * h + 256].reshape(32, 8, 256)
            t.part[:, h] = term if first else t.part[:, h] + term

    add_cross(p.x, True)
    g.start_y()
    g.start_z()
    g.start_x()
    relays = []
    for side in range(2):
        direct[side][side].wait_recv()
        source = lax.rem(p.x + steps[1 - side], 4)
        rows = block.at[source, pl.ds(256 * side, 256)]
        relays.append(send(rows, rows, side_send.at[4 + side], side_recv.at[4 + side], p.at(x=steps[side])))
    for side in range(2):
        direct[side][1 - side].wait_recv()
        add_cross(lax.rem(p.x + steps[1 - side], 4), False)
    g.start_gather_z()
    for r in relays:
        r.wait_recv()
    add_cross(lax.rem(p.x + 2, 4), False)
    t.start_core()
    g.start_gather_y()
    t.start_y()
    g.start_gather_core()
    t.start_z()
    g.finish()
    t.start_gather_z()
    t.start_gather_y()
    t.start_gather_core()
    t.finish()
    for side in range(2):
        for copy in direct[side]:
            copy.wait_send()
        relays[side].wait_send()
    g.drain()
    t.drain()


def scratch(width):
    w = width // 2
    vm = lambda *shape: pltpu.VMEM((*shape, 8, w), F32)
    return [
        vm(32, 2), vm(16, 2), vm(16, 2), vm(3, 4, 2), vm(4, 2), vm(7), vm(), vm(4),
        pltpu.SemaphoreType.DMA((28,)), pltpu.SemaphoreType.DMA((28,)),
    ]


def gather_and_reduce(panel, trailing):
    whole = pl.BlockSpec(memory_space=pltpu.VMEM)
    return pl.pallas_call(
        reduce_kernel,
        out_shape=(
            jax.ShapeDtypeStruct((4, 512, 256), F32),
            jax.ShapeDtypeStruct((32, 2, 8, 128), F32),
            jax.ShapeDtypeStruct((32, 2, 8, 256), F32),
        ),
        in_specs=[pl.BlockSpec(memory_space=pltpu.HBM)] * 2,
        out_specs=(whole,) * 3,
        scratch_shapes=[
            pltpu.VMEM((2048, 512), F32),
            pltpu.SemaphoreType.DMA((2,)),
            pltpu.SemaphoreType.DMA((6,)),
            pltpu.SemaphoreType.DMA((6,)),
            *scratch(256),
            *scratch(512),
        ],
        compiler_params=pltpu.CompilerParams(collective_id=0, has_side_effects=True, vmem_limit_bytes=32 << 20),
    )(panel, trailing)


def row_of(x, j):
    return jnp.broadcast_to(x[j : j + 1, :], x.shape)


def lane_of(x, at):
    return jnp.take_along_axis(x, at, axis=1)


def eight_pivots(k, c, first, a, r, inv):
    sub = lax.broadcasted_iota(jnp.int32, (8, 128), 0)
    lane = lax.broadcasted_iota(jnp.int32, (8, 128), 1)
    start = (k - 16 * c) * 8
    rel = lane - start
    inside = (rel >= 0) & (rel < 8)
    ats = [jnp.zeros((8, 128), jnp.int32) + (start + j) for j in range(8)]
    work = [a[k, h] for h in range(2)]
    d = work[c]
    cols = [lane_of(d, at) for at in ats]
    work[c] = jnp.where(inside, (rel == sub).astype(F32), d)
    work.append(d)
    outs = [jnp.zeros((8, 128), F32) for _ in work]
    for j in range(8):
        pivot = row_of(cols[j], j)
        inverse = 1.0 / pivot
        root = lax.rsqrt(pivot)
        here = sub == j
        for m in range(j + 1, 8):
            term = row_of(cols[m], j) * inverse
            cols[m] = jnp.where(here, term, cols[m] - cols[j] * term)
        for w in range(3):
            row = row_of(work[w], j)
            outs[w] = jnp.where(here, row * root, outs[w])
            term = row * inverse
            work[w] = work[w] - cols[j] * term if w == 2 else jnp.where(here, term, work[w] - cols[j] * term)
    zero = jnp.zeros((8, 128), F32)
    for h in range(2):
        if h == c:
            r[k, h] = jnp.where(rel >= sub, outs[2], 0.0)
            inv[k, h] = jnp.where(rel <= sub, outs[h], 0.0)
        else:
            r[k, h] = outs[h] if h > c else zero
            inv[k, h] = outs[h] if h < c else zero
    rows = [[row_of(work[h], j) for j in range(8)] for h in range(2)]
    for group in range(first, 32):
        old = [a[group, h] for h in range(2)]
        new = list(old)
        new[c] = jnp.where(inside, 0.0, old[c])
        for j in range(8):
            multiplier = lane_of(old[c], ats[j])
            for h in range(2):
                new[h] = new[h] - multiplier * rows[h][j]
        for h in range(2):
            a[group, h] = new[h]


def factor_quarter(q, a, r, inv):
    def step(i, carry):
        eight_pivots(8 * q + i, q // 2, 8 * q, a, r, inv)
        return carry

    lax.fori_loop(0, 8, step, 0)


def factor_kernel(gram, cross, rfactor, projected, weight_high, weight_low, a, r, inv):
    a[...] = gram[...]
    for q in range(4):
        factor_quarter(q, a, r, inv)
    rfactor[...] = halves(r, 256)
    inverse = halves(inv, 256)
    proj = dot(inverse, halves(cross, 512))
    projected[...] = proj
    weight = dot(inverse.T, proj)
    high = weight.astype(jnp.bfloat16)
    weight_high[...] = high
    weight_low[...] = (weight - high.astype(F32)).astype(jnp.bfloat16)


def factor(gram, cross):
    held = pltpu.VMEM((32, 2, 8, 128), F32)
    return pl.pallas_call(
        factor_kernel,
        out_shape=(
            jax.ShapeDtypeStruct((256, 256), F32),
            jax.ShapeDtypeStruct((256, 512), F32),
            jax.ShapeDtypeStruct((256, 512), jnp.bfloat16),
            jax.ShapeDtypeStruct((256, 512), jnp.bfloat16),
        ),
        scratch_shapes=[held, held, held],
        compiler_params=pltpu.CompilerParams(vmem_limit_bytes=16 << 20),
    )(gram, cross)


def update_kernel(trailing, block, weight_high, weight_low, updated):
    x = block[...]
    high = x.astype(jnp.bfloat16)
    low = (x - high.astype(F32)).astype(jnp.bfloat16)
    mul = functools.partial(jnp.dot, preferred_element_type=F32)
    updated[...] = trailing[...] - (mul(high, weight_high[...]) + (mul(high, weight_low[...]) + mul(low, weight_high[...])))


def update(trailing, block, weight_high, weight_low):
    rows = 512
    tile = pl.BlockSpec((rows, 512), lambda i: (i, 0))
    fixed = pl.BlockSpec((256, 512), lambda i: (0, 0))
    return pl.pallas_call(
        update_kernel,
        grid=(2048 // rows,),
        out_shape=jax.ShapeDtypeStruct((2048, 512), F32),
        in_specs=[tile, pl.BlockSpec((rows, 256), lambda i: (i, 0)), fixed, fixed],
        out_specs=tile,
        compiler_params=pltpu.CompilerParams(vmem_limit_bytes=24 << 20),
    )(trailing, block, weight_high, weight_low)


def shards(panel, trailing):
    block, gram, cross = gather_and_reduce(panel, trailing)
    rfactor, projected, high, low = factor(gram, cross)
    return rfactor, projected, update(trailing, block.reshape(2048, 256), high, low)


def solution(mesh):
    return jax.shard_map(
        shards,
        mesh=mesh,
        in_specs=(P(("rows", "cols"), None), P("rows", "cols")),
        out_specs=(P(), P(None, "cols"), P("rows", "cols")),
        check_vma=False,
    )
```

time: 314 us -> 79.9 us (0.25)
  waiting for transfers between devices: 187 us -> 0 us
  Pallas kernels: 0 us -> 75.9 us
  other arithmetic: 55 us -> 0 us
  blocking collectives: 30 us -> 0 us
  matrix products: 18 us -> 0 us
  between operations: 15.6 us -> 0.65 us
  local copies, waits for them, and re-layouts: 7.82 us -> 3.22 us
    psum x1 -> x0, waiting for transfers between devices: 187 us -> none  [in_one(): running = lax.psum(jnp.concatenate([a.ravel() for a in arrays]), axis)]
    pallas_call x0 -> x3, Pallas kernels: none -> 75.9 us  [the longest x1 53.3 us: gather_and_reduce(): pl.pallas_call(reduce_kernel, out_shape=(jax.ShapeDtypeStruct((4, 512, 25...]
    another operation x10 -> x0, other arithmetic: 54 us -> none  [the longest x6 34.1 us: shards(): rfactor = jnp.linalg.cholesky(gram).T]
    all_to_all x1 -> x0, blocking collectives: 30 us -> none  [copy_for_each(): return lax.all_to_all(copies, axis, split_axis=0, concat_axis=0, tiled=True)]
    dot_general x3 -> x0, matrix products: 12.4 us -> none  [the longest x2 7.15 us: inner(): lax.dot_general(left, right, (((0,), (0,)), ((), ())), precision=lax.Prec...]
    another operation x8 -> x0, matrix products: 5.65 us -> none  [the longest x6 5.18 us: lower_solve(): return jax.scipy.linalg.solve_triangular(rfactor.T, right, lower=True)]
    another operation x12 -> x0, local copies, waits for them, and re-layouts: 5.29 us -> none
  transfers between devices with their start and end apart: 1 -> 0, of which waited for: 1 -> 0; matrix products, arithmetic and copies ran while one was open for 0% -> 0% of each run, Pallas kernels for 0% -> 0%
where the time goes in v1:
time: 79.9 us; the launch traced here: 79.7 us
  Pallas kernels  75.9 us (95%)
  local copies, waits for them, and re-layouts  3.22 us (4%)
    pallas_call x1, Pallas kernels, gather_and_reduce(): pl.pallas_call(reduce_kernel, out_shape=(jax.ShapeDtypeStruct((4, 512, 25...  53.3 us
    pallas_call x1, Pallas kernels, factor(): pl.pallas_call(factor_kernel, out_shape=(jax.ShapeDtypeStruct((256, 256),...  18.8 us
    pallas_call x1, Pallas kernels, update(): pl.pallas_call(update_kernel, grid=(2048 // rows,), out_shape=jax.ShapeDt...  3.69 us
    unnamed x4, local copies, waits for them, and re-layouts  3.22 us

profile of v1, /device:TPU:1, one launch (start us, length us, event | category | flops | bytes accessed | tf_op | source)
XLA Modules:
  0.0 79.7 jit_solution(6507954858000464047)
XLA Ops:
  0.6 0.0 copy-start
  0.6 2.2 %copy-done = f32[2048,512]{1,0:T(8,128)S(1)} copy-done((f32[2048,512]{1,0:T(8,128)S(1)}, f32[2048,512]{1,0:T(8,128)}, u32[]{:S(2)}) %copy-start) | copy-done | bytes 4194328
  2.8 0.0 copy-start.1
  2.8 1.0 %copy-done.1 = f32[512,256]{1,0:T(8,128)S(1)} copy-done((f32[512,256]{1,0:T(8,128)S(1)}, f32[512,256]{1,0:T(8,128)}, u32[]{:S(2)}) %copy-start.1) | copy-done | bytes 524312
  3.9 53.3 %shard_map.49 = (f32[4,512,256]{2,1,0:T(8,128)S(1)}, f32[32,2,8,128]{3,2,1,0:T(8,128)S(1)}, f32[32,2,8,256]{3,2,1,0:T(8,128)S(1)}) custom-call(f32[512,256]{1,0:T(8,128)S(1)} %copy-done.1, f32[2048,512]{1,0:T(8,128)S(1)} %copy-done), custom_call_target="tpu_custom_call" | custom-call | tf_op jit(solution)/shard_map/pallas_call | solution.py:217
  57.2 18.8 %shard_map.50 = (f32[256,256]{1,0:T(8,128)}, f32[256,512]{1,0:T(8,128)}, bf16[256,512]{1,0:T(8,128)(2,1)S(1)}, bf16[256,512]{1,0:T(8,128)(2,1)S(1)}) custom-call(f32[32,2,8,128]{3,2,1,0:T(8,128)S(1)} %get-tuple-element.10.gram, f32[32,2,8,256]{3,2,1,0:T(8,128)S(1)} %get-tuple-element.11.cross), custom_call_target="tpu_custom_call" | custom-call | tf_op jit(solution)/shard_map/pallas_call | solution.py:317
  76.0 3.7 %shard_map.51 = f32[2048,512]{1,0:T(8,128)} custom-call(f32[2048,512]{1,0:T(8,128)S(1)} %copy-done, f32[2048,256]{1,0:T(8,128)S(1)} %bitcast.1, bf16[256,512]{1,0:T(8,128)(2,1)S(1)} %get-tuple-element.15.weight_high, bf16[256,512]{1,0:T(8,128)(2,1)S(1)} %get-tuple-element.16.weight_low), custom_call_target="tpu_custom_call" | custom-call | tf_op jit(solution)/shard_map/pallas_call | solution.py:342
Async XLA Ops:
  0.6 2.2 %copy-start = (f32[2048,512]{1,0:T(8,128)S(1)}, f32[2048,512]{1,0:T(8,128)}, u32[]{:S(2)}) copy-start(f32[2048,512]{1,0:T(8,128)} %trailing.3) | copy-start | bytes 12582916
  2.8 1.0 %copy-start.1 = (f32[512,256]{1,0:T(8,128)S(1)}, f32[512,256]{1,0:T(8,128)}, u32[]{:S(2)}) copy-start(f32[512,256]{1,0:T(8,128)} %panel.1) | copy-start | bytes 1572868

commit v2 on v0

v2 whole, which is shorter than its diff:
```python
import functools

import jax
import jax.numpy as jnp
from jax import lax
from jax.experimental import pallas as pl
from jax.experimental.pallas import tpu as pltpu
from jax.sharding import PartitionSpec as P

MESH = pl.DeviceIdType.MESH
HIGHEST = lax.Precision.HIGHEST
F32 = jnp.float32


def dot(left, right):
    return jnp.dot(left, right, precision=HIGHEST, preferred_element_type=F32)


class Place:
    def __init__(self):
        rows = lax.axis_index("rows")
        self.x = lax.axis_index("cols")
        self.core = lax.rem(rows, 2)
        self.z = lax.rem(rows // 2, 8)
        self.y = rows // 16

    def at(self, y=0, z=0, core=0, x=0):
        there = lax.rem(self.y + y, 4) * 16 + lax.rem(self.z + z, 8) * 2 + lax.rem(self.core + core, 2)
        return (there, lax.rem(self.x + x, 4))


def send(src, dst, send_sem, recv_sem, device):
    copy = pltpu.make_async_remote_copy(
        src_ref=src, dst_ref=dst, send_sem=send_sem, recv_sem=recv_sem, device_id=device, device_id_type=MESH
    )
    copy.start()
    return copy


class Reduction:
    def __init__(self, place, refs, over_x):
        self.place, self.over_x = place, over_x
        self.part, self.from_core, self.s1, self.from_y, self.s2, self.from_z, self.s3, self.from_x, self.full = refs[:9]
        self.send_sem, self.recv_sem = refs[9:]
        self.groups, self.across = self.part.shape[:2]
        self.half, self.eighth = self.groups // 2, self.groups // 8
        self.copies = []

    def send(self, src, dst, device):
        used = len(self.copies)
        copy = send(src, dst, self.send_sem.at[used], self.recv_sem.at[used], device)
        self.copies.append(copy)
        return copy

    def start_core(self):
        p = self.place
        self.c1 = self.send(self.part.at[pl.ds(self.half * (1 - p.core), self.half)], self.from_core, p.at(core=1))

    def start_y(self):
        p, n = self.place, self.eighth
        self.c1.wait_recv()
        self.s1[...] = self.part[pl.ds(self.half * p.core, self.half)] + self.from_core[...]
        self.c2 = [self.send(self.s1.at[pl.ds(n * lax.rem(p.y + d, 4), n)], self.from_y.at[d - 1], p.at(y=d)) for d in (2, 1, 3)]

    def start_z(self):
        p, n = self.place, self.eighth
        for c in self.c2:
            c.wait_recv()
        self.s2[...] = (self.s1[pl.ds(n * p.y, n)] + self.from_y[0]) + (self.from_y[1] + self.from_y[2])
        self.c3 = []
        for d in (4, 3, 5, 2, 6, 1, 7):
            there = lax.rem(p.z + d, 8)
            self.c3.append(self.send(self.s2.at[there // self.across, lax.rem(there, self.across)], self.from_z.at[d - 1], p.at(z=d)))

    def end_z(self):
        p = self.place
        for c in self.c3:
            c.wait_recv()
        f = self.from_z
        total = self.s2[p.z // self.across, lax.rem(p.z, self.across)]
        return ((total + f[0]) + (f[1] + f[2])) + ((f[3] + f[4]) + (f[5] + f[6]))

    def start_x(self):
        p = self.place
        self.s3[...] = self.end_z()
        self.c4 = [self.send(self.s3, self.from_x.at[p.x], p.at(x=d)) for d in (2, 1, 3)]
        self.from_x[p.x] = self.s3[...]

    def start_gather_z(self):
        p = self.place
        group, across = self.half * p.core + self.eighth * p.y + p.z // self.across, lax.rem(p.z, self.across)
        if self.over_x:
            for c in self.c4:
                c.wait_recv()
            self.full[group, across] = (self.from_x[0] + self.from_x[1]) + (self.from_x[2] + self.from_x[3])
        else:
            self.full[group, across] = self.end_z()
        mine = self.full.at[group, across]
        self.c5 = [self.send(mine, mine, p.at(z=d)) for d in (4, 3, 5, 2, 6, 1, 7)]

    def block(self, y):
        return self.full.at[pl.ds(self.half * self.place.core + self.eighth * y, self.eighth)]

    def start_gather_y(self):
        p = self.place
        for c in self.c5:
            c.wait_recv()
        mine = self.block(p.y)
        self.c6 = [self.send(mine, mine, p.at(y=d)) for d in (2, 1, 3)]
        self.c7 = [self.send(mine, mine, p.at(core=1))]

    def start_gather_core(self):
        p = self.place
        for c, d in zip(self.c6, (2, 1, 3)):
            c.wait_recv()
            theirs = self.block(lax.rem(p.y + 4 - d, 4))
            self.c7.append(self.send(theirs, theirs, p.at(core=1)))

    def finish(self):
        for c in self.c7:
            c.wait_recv()

    def drain(self):
        for c in self.copies:
            c.wait_send()


def tiled(matrix):
    n = matrix.shape[0] // 8
    return [matrix[:, 128 * h : 128 * h + 128].reshape(n, 8, 128) for h in range(matrix.shape[1] // 128)]


def whole(ref):
    n, m = ref.shape[:2]
    return jnp.concatenate([ref[:, h].reshape(8 * n, 128) for h in range(m)], axis=1)


def row_of(x, j):
    return jnp.broadcast_to(x[j : j + 1, :], x.shape)


def lane_of(x, at):
    return jnp.take_along_axis(x, at, axis=1)


def eight_pivots(k, base, a, r, inv):
    sub = lax.broadcasted_iota(jnp.int32, (8, 128), 0)
    lane = lax.broadcasted_iota(jnp.int32, (8, 128), 1)
    rel = [lane + (128 * h - 8 * k) for h in range(2)]
    inside = [(x >= 0) & (x < 8) for x in rel]
    c = k // 16
    start = 8 * lax.rem(k, 16)
    ats = [jnp.zeros((8, 128), jnp.int32) + (start + j) for j in range(8)]
    d = a[k, c]
    cols = [lane_of(d, at) for at in ats]
    work = [jnp.where(inside[h], (rel[h] == sub).astype(F32), a[k, h]) for h in range(2)] + [d]
    outs = [jnp.zeros((8, 128), F32) for _ in work]
    for j in range(8):
        here = sub == j
        root = lax.rsqrt(row_of(cols[j], j))
        scaled = cols[j] * root
        for m in range(j + 1, 8):
            term = row_of(cols[m], j) * root
            cols[m] = jnp.where(here, term * root, cols[m] - scaled * term)
        for w in range(3):
            term = row_of(work[w], j) * root
            outs[w] = jnp.where(here, term, outs[w])
            rest = work[w] - scaled * term
            work[w] = rest if w == 2 else jnp.where(here, term * root, rest)
    for h in range(2):
        r[k, h] = jnp.where(rel[h] >= 8, outs[h], jnp.where(inside[h] & (rel[h] >= sub), outs[2], 0.0))
        inv[k, h] = jnp.where(rel[h] <= sub, outs[h], 0.0)
    rows = [[row_of(work[h], j) for j in range(8)] for h in range(2)]
    source = [a[base + g, c] for g in range(8)]
    new = [[jnp.where(inside[h], 0.0, a[base + g, h]) for h in range(2)] for g in range(8)]
    for j in range(8):
        for g in range(8):
            multiplier = lane_of(source[g], ats[j])
            for h in range(2):
                new[g][h] = new[g][h] - multiplier * rows[h][j]
    for g in range(8):
        for h in range(2):
            a[base + g, h] = new[g][h]


def take_out(s, a, r, inv):
    base = 8 * s
    rows = lambda ref, h: ref[pl.ds(base, 8), h].reshape(64, 128)
    right = []
    for h in range(2):
        col = lax.broadcasted_iota(jnp.int32, (64, 128), 1) + 128 * h
        right.append(jnp.where(col < 64 * (s + 1), rows(inv, h), rows(r, h)))
    right = jnp.concatenate(right, axis=1)
    for half in range((s + 1) // 2, 2):
        product = tiled(dot(rows(r, half).T, right))
        for h in range(2):
            col = lax.broadcasted_iota(jnp.int32, (16, 8, 128), 2) + 128 * h
            old = a[pl.ds(16 * half, 16), h]
            a[pl.ds(16 * half, 16), h] = jnp.where((col >= 64 * s) & (col < 64 * (s + 1)), 0.0, old) - product[h]


def factor_part(eighth, a, r, inv):
    s = eighth // 2

    def step(i, carry):
        eight_pivots(4 * eighth + i, 8 * s, a, r, inv)
        return carry

    lax.fori_loop(0, 4, step, 0)
    if eighth % 2 and s < 3:
        take_out(s, a, r, inv)


def split(x):
    high = x.astype(jnp.bfloat16)
    return high, (x - high.astype(F32)).astype(jnp.bfloat16)


def main_kernel(
    panel, trailing, block_high, block_low, rfactor, projected, weight_high, weight_low,
    block, held, a, inv, r, load_sem, side_send, side_recv, *rest
):
    p = Place()
    g = Reduction(p, rest[:11], True)
    t = [Reduction(p, rest[11 + 11 * q : 22 + 11 * q], False) for q in range(2)]

    own = pltpu.make_async_copy(panel, block.at[p.x], load_sem.at[0])
    own.start()
    load = pltpu.make_async_copy(trailing, held, load_sem.at[1])
    load.start()

    barrier = pltpu.get_barrier_semaphore()
    peers = [p.at(core=1)] + [p.at(y=d) for d in (1, 2, 3)] + [p.at(z=d) for d in range(1, 8)] + [p.at(x=d) for d in (1, 2, 3)]
    for peer in peers:
        pl.semaphore_signal(barrier, inc=1, device_id=peer, device_id_type=MESH)
    pl.semaphore_wait(barrier, len(peers))
    own.wait()

    steps = (1, 3)
    x_copies = []

    def side_copy(source, q, half, side, slot):
        rows = block.at[source, pl.ds(256 * half, 256), pl.ds(128 * q, 128)]
        at = 6 * q + 2 * slot + side
        copy = send(rows, rows, side_send.at[at], side_recv.at[at], p.at(x=steps[side]))
        x_copies.append(copy)
        return copy

    def direct(q, n):
        return [side_copy(p.x, q, n if side == 0 else 1 - n, side, n) for side in range(2)]

    def relay(q, arrived):
        copies = []
        for side in range(2):
            arrived[side].wait_recv()
            copies.append(side_copy(lax.rem(p.x + steps[1 - side], 4), q, side, side, 2))
        return copies

    def wait(copies):
        for copy in copies:
            copy.wait_recv()

    def add_cross(q, step, first=False):
        x = lax.rem(p.x + step, 4)
        terms = tiled(dot(block[x, :, 128 * q : 128 * q + 128].T, held[pl.ds(512 * x, 512), :]))
        for h in range(4):
            t[q].part[:, h] = terms[h] if first else t[q].part[:, h] + terms[h]

    first0 = direct(0, 0)
    second0 = direct(0, 1)
    mine = block[p.x]
    for h, tile in enumerate(tiled(dot(mine.T, mine))):
        g.part[:, h] = tile
    g.start_core()
    load.wait()
    add_cross(0, 0, True)
    g.start_y()
    relay0 = relay(0, first0)
    first1 = direct(1, 0)
    add_cross(1, 0, True)
    g.start_z()
    wait(second0)
    add_cross(0, 1)
    add_cross(0, 3)
    g.start_x()
    second1 = direct(1, 1)
    wait(relay0)
    add_cross(0, 2)
    t[0].start_core()
    t[0].start_y()
    relay1 = relay(1, first1)
    g.start_gather_z()
    wait(second1)
    add_cross(1, 1)
    add_cross(1, 3)
    t[0].start_z()
    g.start_gather_y()
    wait(relay1)
    add_cross(1, 2)
    t[1].start_core()
    for x in range(4):
        rows = pl.ds(512 * x, 512)
        block_high[rows, :], block_low[rows, :] = split(block[x])
    g.start_gather_core()
    t[1].start_y()
    g.finish()
    a[...] = g.full[...]
    factor_part(0, a, r, inv)
    t[0].start_gather_z()
    factor_part(1, a, r, inv)
    t[1].start_z()
    factor_part(2, a, r, inv)
    factor_part(3, a, r, inv)
    t[0].start_gather_y()
    factor_part(4, a, r, inv)
    t[1].start_gather_z()
    factor_part(5, a, r, inv)
    t[0].start_gather_core()
    factor_part(6, a, r, inv)
    factor_part(7, a, r, inv)
    t[1].start_gather_y()
    rfactor[...] = whole(r)
    inverse = whole(inv)
    t[0].finish()
    proj = dot(inverse[:, :128], whole(t[0].full))
    t[1].start_gather_core()
    t[1].finish()
    proj = proj + dot(inverse[:, 128:], whole(t[1].full))
    projected[...] = proj
    weight_high[...], weight_low[...] = split(dot(inverse.T, proj))
    for copy in x_copies:
        copy.wait_send()
    for reduction in (g, *t):
        reduction.drain()


def scratch(groups, across):
    tiles = lambda *shape: pltpu.VMEM((*shape, 8, 128), F32)
    return [
        tiles(groups, across), tiles(groups // 2, across), tiles(groups // 2, across), tiles(3, groups // 8, across),
        tiles(groups // 8, across), tiles(7), tiles(), tiles(4), tiles(groups, across),
        pltpu.SemaphoreType.DMA((28,)), pltpu.SemaphoreType.DMA((28,)),
    ]


def main_part(panel, trailing):
    inner = pl.BlockSpec(memory_space=pltpu.VMEM)
    halves = pltpu.VMEM((32, 2, 8, 128), F32)
    return pl.pallas_call(
        main_kernel,
        out_shape=(
            jax.ShapeDtypeStruct((2048, 256), jnp.bfloat16),
            jax.ShapeDtypeStruct((2048, 256), jnp.bfloat16),
            jax.ShapeDtypeStruct((256, 256), F32),
            jax.ShapeDtypeStruct((256, 512), F32),
            jax.ShapeDtypeStruct((256, 512), jnp.bfloat16),
            jax.ShapeDtypeStruct((256, 512), jnp.bfloat16),
        ),
        in_specs=[pl.BlockSpec(memory_space=pltpu.HBM)] * 2,
        out_specs=(inner,) * 6,
        scratch_shapes=[
            pltpu.VMEM((4, 512, 256), F32),
            pltpu.VMEM((2048, 512), F32),
            halves,
            halves,
            halves,
            pltpu.SemaphoreType.DMA((2,)),
            pltpu.SemaphoreType.DMA((12,)),
            pltpu.SemaphoreType.DMA((12,)),
            *scratch(32, 2),
            *scratch(16, 4),
            *scratch(16, 4),
        ],
        compiler_params=pltpu.CompilerParams(collective_id=0, has_side_effects=True, vmem_limit_bytes=50 << 20),
    )(panel, trailing)


def update_kernel(trailing, high, low, weight_high, weight_low, rfactor, projected, rfactor_out, projected_out, updated):
    @pl.when(pl.program_id(0) == 0)
    def _():
        rfactor_out[...] = rfactor[...]
        projected_out[...] = projected[...]

    mul = functools.partial(jnp.dot, preferred_element_type=F32)
    x = high[...]
    updated[...] = trailing[...] - (mul(x, weight_high[...]) + (mul(x, weight_low[...]) + mul(low[...], weight_high[...])))


def update(trailing, high, low, weight_high, weight_low, rfactor, projected):
    rows = 256
    tile = pl.BlockSpec((rows, 512), lambda i: (i, 0))
    part = pl.BlockSpec((rows, 256), lambda i: (i, 0))
    fixed = pl.BlockSpec((256, 512), lambda i: (0, 0))
    square = pl.BlockSpec((256, 256), lambda i: (0, 0))
    return pl.pallas_call(
        update_kernel,
        grid=(2048 // rows,),
        out_shape=(
            jax.ShapeDtypeStruct((256, 256), F32),
            jax.ShapeDtypeStruct((256, 512), F32),
            jax.ShapeDtypeStruct((2048, 512), F32),
        ),
        in_specs=[tile, part, part, fixed, fixed, square, fixed],
        out_specs=(square, fixed, tile),
        compiler_params=pltpu.CompilerParams(vmem_limit_bytes=24 << 20),
    )(trailing, high, low, weight_high, weight_low, rfactor, projected)


def shards(panel, trailing):
    high, low, rfactor, projected, weight_high, weight_low = main_part(pltpu.with_memory_space_constraint(panel, pltpu.HBM), trailing)
    return update(trailing, high, low, weight_high, weight_low, rfactor, projected)


def solution(mesh):
    return jax.shard_map(
        shards,
        mesh=mesh,
        in_specs=(P(("rows", "cols"), None), P("rows", "cols")),
        out_specs=(P(), P(None, "cols"), P("rows", "cols")),
        check_vma=False,
    )
```

time: 314 us -> 61.8 us (0.20)
  waiting for transfers between devices: 187 us -> 0 us
  Pallas kernels: 0 us -> 61.1 us
  other arithmetic: 55 us -> 0 us
  blocking collectives: 30 us -> 0 us
  matrix products: 18 us -> 0 us
  between operations: 15.6 us -> 0.65 us
  local copies, waits for them, and re-layouts: 7.82 us -> 0.01 us
    psum x1 -> x0, waiting for transfers between devices: 187 us -> none  [in_one(): running = lax.psum(jnp.concatenate([a.ravel() for a in arrays]), axis)]
    pallas_call x0 -> x2, Pallas kernels: none -> 61.1 us  [the longest x1 55.9 us: main_part(): pl.pallas_call(main_kernel, out_shape=(jax.ShapeDtypeStruct((2048, 256),...]
    another operation x10 -> x0, other arithmetic: 54 us -> none  [the longest x6 34.1 us: shards(): rfactor = jnp.linalg.cholesky(gram).T]
    all_to_all x1 -> x0, blocking collectives: 30 us -> none  [copy_for_each(): return lax.all_to_all(copies, axis, split_axis=0, concat_axis=0, tiled=True)]
    dot_general x3 -> x0, matrix products: 12.4 us -> none  [the longest x2 7.15 us: inner(): lax.dot_general(left, right, (((0,), (0,)), ((), ())), precision=lax.Prec...]
    another operation x8 -> x0, matrix products: 5.65 us -> none  [the longest x6 5.18 us: lower_solve(): return jax.scipy.linalg.solve_triangular(rfactor.T, right, lower=True)]
    another operation x12 -> x0, local copies, waits for them, and re-layouts: 5.29 us -> none
  transfers between devices with their start and end apart: 1 -> 0, of which waited for: 1 -> 0; matrix products, arithmetic and copies ran while one was open for 0% -> 0% of each run, Pallas kernels for 0% -> 0%
where the time goes in v2:
time: 61.8 us; the launch traced here: 61.7 us
  Pallas kernels  61.1 us (99%)
  between operations  0.65 us (1%)
    pallas_call x1, Pallas kernels, main_part(): pl.pallas_call(main_kernel, out_shape=(jax.ShapeDtypeStruct((2048, 256),...  55.9 us
    pallas_call x1, Pallas kernels, update(): pl.pallas_call(update_kernel, grid=(2048 // rows,), out_shape=(jax.ShapeD...  5.16 us

profile of v2, /device:TPU:1, one launch (start us, length us, event | category | flops | bytes accessed | tf_op | source)
XLA Modules:
  0.0 61.7 jit_solution(17396564183276846378)
XLA Ops:
  0.6 0.0 copy-start
  0.6 55.9 %shard_map.49 = (bf16[2048,256]{1,0:T(8,128)(2,1)S(1)}, bf16[2048,256]{1,0:T(8,128)(2,1)S(1)}, f32[256,256]{1,0:T(8,128)S(1)}, f32[256,512]{1,0:T(8,128)S(1)}, b...) custom-call(f32[512,256]{1,0:T(8,128)} %panel.1, f32[2048,512]{1,0:T(8,128)} %trailing.3), custom_call_target="tpu_custom_call" | custom-call | tf_op jit(solution)/shard_map/pallas_call | solution.py:349
  56.6 0.0 copy-done
  56.6 5.2 %shard_map.50 = (f32[256,256]{1,0:T(8,128)}, f32[256,512]{1,0:T(8,128)}, f32[2048,512]{1,0:T(8,128)}) custom-call(f32[2048,512]{1,0:T(8,128)S(1)} %copy-done, bf16[2048,256]{1,0:T(8,128)(2,1)S(1)} %get-tuple-element.9.high, bf16[2048,256]{1,0:T(8,128)(2,1)S(1)} %get-tuple-element.10.low, bf16[256,512]{1,0:T(8,128)(2,1)S(1)} %get-tuple-element.11.weight_high, ...), custom_call_target="tpu_custom_call" | custom-call | tf_op jit(solution)/shard_map/pallas_call | solution.py:395
Async XLA Ops:
  0.6 55.9 %copy-start = (f32[2048,512]{1,0:T(8,128)S(1)}, f32[2048,512]{1,0:T(8,128)}, u32[]{:S(2)}) copy-start(f32[2048,512]{1,0:T(8,128)} %trailing.3) | copy-start | bytes 12582916

commit v3 on v2

--- a/solution.py
+++ b/solution.py
@@ -37,11 +37,16 @@
     return copy
 
 
+PLANE = sorted(
+    [(y, z) for y in range(4) for z in range(8) if (y, z) != (0, 0)], key=lambda d: (-min(d[0], 4 - d[0]) - min(d[1], 8 - d[1]), d)
+)
+
+
 class Reduction:
     def __init__(self, place, refs, over_x):
         self.place, self.over_x = place, over_x
-        self.part, self.from_core, self.s1, self.from_y, self.s2, self.from_z, self.s3, self.from_x, self.full = refs[:9]
-        self.send_sem, self.recv_sem = refs[9:]
+        self.part, self.from_core, self.s1, self.from_y, self.s2, self.from_z, self.from_plane, self.s3, self.from_x, self.full = refs[:10]
+        self.send_sem, self.recv_sem = refs[10:]
         self.groups, self.across = self.part.shape[:2]
         self.half, self.eighth = self.groups // 2, self.groups // 8
         self.copies = []
@@ -61,6 +66,27 @@
         self.c1.wait_recv()
         self.s1[...] = self.part[pl.ds(self.half * p.core, self.half)] + self.from_core[...]
         self.c2 = [self.send(self.s1.at[pl.ds(n * lax.rem(p.y + d, 4), n)], self.from_y.at[d - 1], p.at(y=d)) for d in (2, 1, 3)]
+
+    def tile(self, y, z):
+        return self.eighth * y + z // self.across, lax.rem(z, self.across)
+
+    def start_plane(self):
+        p = self.place
+        self.c1.wait_recv()
+        self.s1[...] = self.part[pl.ds(self.half * p.core, self.half)] + self.from_core[...]
+        self.c3 = []
+        for n, (y, z) in enumerate(PLANE):
+            there = self.tile(lax.rem(p.y + y, 4), lax.rem(p.z + z, 8))
+            self.c3.append(self.send(self.s1.at[there], self.from_plane.at[n], p.at(y=y, z=z)))
+
+    def end_plane(self):
+        terms = [self.s1[self.tile(self.place.y, self.place.z)]]
+        for n in reversed(range(len(PLANE))):
+            self.c3[n].wait_recv()
+            terms.append(self.from_plane[n])
+        while len(terms) > 1:
+            terms = [a + b for a, b in zip(terms[::2], terms[1::2])]
+        return terms[0]
 
     def start_z(self):
         p, n = self.place, self.eighth
@@ -86,35 +112,28 @@
         self.c4 = [self.send(self.s3, self.from_x.at[p.x], p.at(x=d)) for d in (2, 1, 3)]
         self.from_x[p.x] = self.s3[...]
 
-    def start_gather_z(self):
-        p = self.place
-        group, across = self.half * p.core + self.eighth * p.y + p.z // self.across, lax.rem(p.z, self.across)
+    def start_gather(self):
+        p = self.place
+        group, across = self.tile(p.y, p.z)
+        group = self.half * p.core + group
         if self.over_x:
             for c in self.c4:
                 c.wait_recv()
             self.full[group, across] = (self.from_x[0] + self.from_x[1]) + (self.from_x[2] + self.from_x[3])
         else:
-            self.full[group, across] = self.end_z()
+            self.full[group, across] = self.end_plane()
         mine = self.full.at[group, across]
-        self.c5 = [self.send(mine, mine, p.at(z=d)) for d in (4, 3, 5, 2, 6, 1, 7)]
-
-    def block(self, y):
-        return self.full.at[pl.ds(self.half * self.place.core + self.eighth * y, self.eighth)]
-
-    def start_gather_y(self):
-        p = self.place
-        for c in self.c5:
-            c.wait_recv()
-        mine = self.block(p.y)
-        self.c6 = [self.send(mine, mine, p.at(y=d)) for d in (2, 1, 3)]
-        self.c7 = [self.send(mine, mine, p.at(core=1))]
+        self.c5 = [self.send(mine, mine, p.at(y=y, z=z)) for y, z in PLANE]
 
     def start_gather_core(self):
         p = self.place
-        for c, d in zip(self.c6, (2, 1, 3)):
-            c.wait_recv()
-            theirs = self.block(lax.rem(p.y + 4 - d, 4))
-            self.c7.append(self.send(theirs, theirs, p.at(core=1)))
+        self.c7 = []
+        for step in (0, 1, 3, 2):
+            for c, (y, z) in zip(self.c5, PLANE):
+                if y == (4 - step) % 4:
+                    c.wait_recv()
+            rows = self.full.at[pl.ds(self.half * p.core + self.eighth * lax.rem(p.y + step, 4), self.eighth)]
+            self.c7.append(self.send(rows, rows, p.at(core=1)))
 
     def finish(self):
         for c in self.c7:
@@ -217,30 +236,34 @@
 
 
 def main_kernel(
-    panel, trailing, block_high, block_low, rfactor, projected, weight_high, weight_low,
-    block, held, a, inv, r, load_sem, side_send, side_recv, *rest
+    panel, trailing, block_high, block_low, rfactor, projected, weight_high, weight_low, held,
+    block, a, inv, r, load_sem, side_send, side_recv, *rest
 ):
     p = Place()
-    g = Reduction(p, rest[:11], True)
-    t = [Reduction(p, rest[11 + 11 * q : 22 + 11 * q], False) for q in range(2)]
-
-    own = pltpu.make_async_copy(panel, block.at[p.x], load_sem.at[0])
-    own.start()
-    load = pltpu.make_async_copy(trailing, held, load_sem.at[1])
-    load.start()
+    g = Reduction(p, rest[:12], True)
+    t = [Reduction(p, rest[12 + 12 * q : 24 + 12 * q], False) for q in range(2)]
+
+    owns = [
+        pltpu.make_async_copy(panel.at[:, pl.ds(128 * q, 128)], block.at[p.x, q], load_sem.at[q]) for q in range(2)
+    ]
+    for own in owns:
+        own.start()
+    load = pltpu.make_async_copy(trailing, held, load_sem.at[2])
 
     barrier = pltpu.get_barrier_semaphore()
     peers = [p.at(core=1)] + [p.at(y=d) for d in (1, 2, 3)] + [p.at(z=d) for d in range(1, 8)] + [p.at(x=d) for d in (1, 2, 3)]
     for peer in peers:
         pl.semaphore_signal(barrier, inc=1, device_id=peer, device_id_type=MESH)
     pl.semaphore_wait(barrier, len(peers))
-    own.wait()
+    for own in owns:
+        own.wait()
+    load.start()
 
     steps = (1, 3)
     x_copies = []
 
     def side_copy(source, q, half, side, slot):
-        rows = block.at[source, pl.ds(256 * half, 256), pl.ds(128 * q, 128)]
+        rows = block.at[source, q, pl.ds(256 * half, 256)]
         at = 6 * q + 2 * slot + side
         copy = send(rows, rows, side_send.at[at], side_recv.at[at], p.at(x=steps[side]))
         x_copies.append(copy)
@@ -262,13 +285,13 @@
 
     def add_cross(q, step, first=False):
         x = lax.rem(p.x + step, 4)
-        terms = tiled(dot(block[x, :, 128 * q : 128 * q + 128].T, held[pl.ds(512 * x, 512), :]))
+        terms = tiled(dot(block[x, q].T, held[pl.ds(512 * x, 512), :]))
         for h in range(4):
             t[q].part[:, h] = terms[h] if first else t[q].part[:, h] + terms[h]
 
     first0 = direct(0, 0)
     second0 = direct(0, 1)
-    mine = block[p.x]
+    mine = jnp.concatenate([block[p.x, q] for q in range(2)], axis=1)
     for h, tile in enumerate(tiled(dot(mine.T, mine))):
         g.part[:, h] = tile
     g.start_core()
@@ -287,47 +310,46 @@
     wait(relay0)
     add_cross(0, 2)
     t[0].start_core()
-    t[0].start_y()
     relay1 = relay(1, first1)
-    g.start_gather_z()
+    t[0].start_plane()
+    g.start_gather()
     wait(second1)
     add_cross(1, 1)
     add_cross(1, 3)
-    t[0].start_z()
-    g.start_gather_y()
     wait(relay1)
     add_cross(1, 2)
     t[1].start_core()
-    for x in range(4):
-        rows = pl.ds(512 * x, 512)
-        block_high[rows, :], block_low[rows, :] = split(block[x])
     g.start_gather_core()
-    t[1].start_y()
+    t[1].start_plane()
+    t[0].start_gather()
     g.finish()
     a[...] = g.full[...]
     factor_part(0, a, r, inv)
-    t[0].start_gather_z()
     factor_part(1, a, r, inv)
-    t[1].start_z()
     factor_part(2, a, r, inv)
+    t[1].start_gather()
     factor_part(3, a, r, inv)
-    t[0].start_gather_y()
+    t[0].start_gather_core()
+    for x in range(4):
+        for q in range(2):
+            at = (pl.ds(512 * x, 512), pl.ds(128 * q, 128))
+            block_high[at], block_low[at] = split(block[x, q])
     factor_part(4, a, r, inv)
-    t[1].start_gather_z()
     factor_part(5, a, r, inv)
-    t[0].start_gather_core()
     factor_part(6, a, r, inv)
     factor_part(7, a, r, inv)
-    t[1].start_gather_y()
     rfactor[...] = whole(r)
     inverse = whole(inv)
+    square = dot(inverse.T, inverse)
     t[0].finish()
-    proj = dot(inverse[:, :128], whole(t[0].full))
+    upper = whole(t[0].full)
+    projected[...] = dot(inverse[:, :128], upper)
+    weight = dot(square[:, :128], upper)
     t[1].start_gather_core()
     t[1].finish()
-    proj = proj + dot(inverse[:, 128:], whole(t[1].full))
-    projected[...] = proj
-    weight_high[...], weight_low[...] = split(dot(inverse.T, proj))
+    lower = whole(t[1].full)
+    weight_high[...], weight_low[...] = split(weight + dot(square[:, 128:], lower))
+    projected[128:, :] = projected[128:, :] + dot(inverse[128:, 128:], lower)
     for copy in x_copies:
         copy.wait_send()
     for reduction in (g, *t):
@@ -338,8 +360,8 @@
     tiles = lambda *shape: pltpu.VMEM((*shape, 8, 128), F32)
     return [
         tiles(groups, across), tiles(groups // 2, across), tiles(groups // 2, across), tiles(3, groups // 8, across),
-        tiles(groups // 8, across), tiles(7), tiles(), tiles(4), tiles(groups, across),
-        pltpu.SemaphoreType.DMA((28,)), pltpu.SemaphoreType.DMA((28,)),
+        tiles(groups // 8, across), tiles(7), tiles(len(PLANE)), tiles(), tiles(4), tiles(groups, across),
+        pltpu.SemaphoreType.DMA((72,)), pltpu.SemaphoreType.DMA((72,)),
     ]
 
 
@@ -355,60 +377,70 @@
             jax.ShapeDtypeStruct((256, 512), F32),
             jax.ShapeDtypeStruct((256, 512), jnp.bfloat16),
             jax.ShapeDtypeStruct((256, 512), jnp.bfloat16),
+            jax.ShapeDtypeStruct((2048, 512), F32),
         ),
         in_specs=[pl.BlockSpec(memory_space=pltpu.HBM)] * 2,
-        out_specs=(inner,) * 6,
+        out_specs=(inner,) * 7,
         scratch_shapes=[
-            pltpu.VMEM((4, 512, 256), F32),
-            pltpu.VMEM((2048, 512), F32),
+            pltpu.VMEM((4, 2, 512, 128), F32),
             halves,
             halves,
             halves,
-            pltpu.SemaphoreType.DMA((2,)),
+            pltpu.SemaphoreType.DMA((3,)),
             pltpu.SemaphoreType.DMA((12,)),
             pltpu.SemaphoreType.DMA((12,)),
             *scratch(32, 2),
             *scratch(16, 4),
             *scratch(16, 4),
         ],
-        compiler_params=pltpu.CompilerParams(collective_id=0, has_side_effects=True, vmem_limit_bytes=50 << 20),
+        compiler_params=pltpu.CompilerParams(collective_id=0, has_side_effects=True, vmem_limit_bytes=40 << 20),
     )(panel, trailing)
 
 
-def update_kernel(trailing, high, low, weight_high, weight_low, rfactor, projected, rfactor_out, projected_out, updated):
-    @pl.when(pl.program_id(0) == 0)
-    def _():
-        rfactor_out[...] = rfactor[...]
-        projected_out[...] = projected[...]
-
+ROWS = 256
+
+
+def update_kernel(held, high, low, weight_high, weight_low, rfactor, projected, rfactor_out, projected_out, updated, tiles, sems):
+    n = 2048 // ROWS
+    copies = [
+        pltpu.make_async_copy(rfactor, rfactor_out, sems.at[n]),
+        pltpu.make_async_copy(projected, projected_out, sems.at[n + 1]),
+    ]
+    for copy in copies:
+        copy.start()
     mul = functools.partial(jnp.dot, preferred_element_type=F32)
-    x = high[...]
-    updated[...] = trailing[...] - (mul(x, weight_high[...]) + (mul(x, weight_low[...]) + mul(low[...], weight_high[...])))
-
-
-def update(trailing, high, low, weight_high, weight_low, rfactor, projected):
-    rows = 256
-    tile = pl.BlockSpec((rows, 512), lambda i: (i, 0))
-    part = pl.BlockSpec((rows, 256), lambda i: (i, 0))
-    fixed = pl.BlockSpec((256, 512), lambda i: (0, 0))
-    square = pl.BlockSpec((256, 256), lambda i: (0, 0))
+    for i in range(n):
+        rows = pl.ds(ROWS * i, ROWS)
+        x = high[rows, :]
+        product = mul(x, weight_high[...]) + (mul(x, weight_low[...]) + mul(low[rows, :], weight_high[...]))
+        tiles[i] = held[rows, :] - product
+        copy = pltpu.make_async_copy(tiles.at[i], updated.at[rows], sems.at[i])
+        copy.start()
+        copies.append(copy)
+    for copy in copies:
+        copy.wait()
+
+
+def update(*operands):
+    inner, outer = pl.BlockSpec(memory_space=pltpu.VMEM), pl.BlockSpec(memory_space=pltpu.HBM)
     return pl.pallas_call(
         update_kernel,
-        grid=(2048 // rows,),
         out_shape=(
             jax.ShapeDtypeStruct((256, 256), F32),
             jax.ShapeDtypeStruct((256, 512), F32),
             jax.ShapeDtypeStruct((2048, 512), F32),
         ),
-        in_specs=[tile, part, part, fixed, fixed, square, fixed],
-        out_specs=(square, fixed, tile),
+        in_specs=[inner] * 7,
+        out_specs=(outer,) * 3,
+        scratch_shapes=[pltpu.VMEM((2048 // ROWS, ROWS, 512), F32), pltpu.SemaphoreType.DMA((2048 // ROWS + 2,))],
         compiler_params=pltpu.CompilerParams(vmem_limit_bytes=24 << 20),
-    )(trailing, high, low, weight_high, weight_low, rfactor, projected)
+    )(*operands)
 
 
 def shards(panel, trailing):
-    high, low, rfactor, projected, weight_high, weight_low = main_part(pltpu.with_memory_space_constraint(panel, pltpu.HBM), trailing)
-    return update(trailing, high, low, weight_high, weight_low, rfactor, projected)
+    outside = [pltpu.with_memory_space_constraint(x, pltpu.HBM) for x in (panel, trailing)]
+    high, low, rfactor, projected, weight_high, weight_low, held = main_part(*outside)
+    return update(held, high, low, weight_high, weight_low, rfactor, projected)
 
 
 def solution(mesh):

time: 61.8 us -> 58.8 us (0.951)
  Pallas kernels: 61.1 us -> 57.9 us
    pallas_call x1, Pallas kernels: 5.16 us -> 2.68 us  [update(): pl.pallas_call(update_kernel, out_shape=(jax.ShapeDtypeStruct((256, 256),...]
    pallas_call x1, Pallas kernels: 55.9 us -> 55.2 us  [main_part(): pl.pallas_call(main_kernel, out_shape=(jax.ShapeDtypeStruct((2048, 256),...]
where the time goes in v3:
time: 58.8 us; the launch traced here: 58.7 us
  Pallas kernels  57.9 us (98%)
  between operations  0.8 us (1%)
    pallas_call x1, Pallas kernels, main_part(): pl.pallas_call(main_kernel, out_shape=(jax.ShapeDtypeStruct((2048, 256),...  55.2 us
    pallas_call x1, Pallas kernels, update(): pl.pallas_call(update_kernel, out_shape=(jax.ShapeDtypeStruct((256, 256),...  2.68 us

profile of v3, /device:TPU:1, one launch (start us, length us, event | category | flops | bytes accessed | tf_op | source)
XLA Modules:
  0.0 58.7 jit_solution(984832407466500681)
XLA Ops:
  0.6 55.2 %shard_map.49 = (bf16[2048,256]{1,0:T(8,128)(2,1)S(1)}, bf16[2048,256]{1,0:T(8,128)(2,1)S(1)}, f32[256,256]{1,0:T(8,128)S(1)}, f32[256,512]{1,0:T(8,128)S(1)}, b...) custom-call(f32[512,256]{1,0:T(8,128)} %panel.1, f32[2048,512]{1,0:T(8,128)} %trailing.1), custom_call_target="tpu_custom_call" | custom-call | tf_op jit(solution)/shard_map/pallas_call | solution.py:371
  55.9 2.7 %shard_map.50 = (f32[256,256]{1,0:T(8,128)}, f32[256,512]{1,0:T(8,128)}, f32[2048,512]{1,0:T(8,128)}) custom-call(f32[2048,512]{1,0:T(8,128)S(1)} %get-tuple-element.10.held, bf16[2048,256]{1,0:T(8,128)(2,1)S(1)} %get-tuple-element.11.high, bf16[2048,256]{1,0:T(8,128)(2,1)S(1)} %get-tuple-element.12.low, bf16[256,512]{1,0:T(8,128)(2,1)S(1)} %get-tuple-element.13.weight_high, ...), custom_call_target="tpu_custom_call" | custom-call | tf_op jit(solution)/shard_map/pallas_call | solution.py:426

commit v4 on v3

--- a/solution.py
+++ b/solution.py
@@ -49,59 +49,63 @@
         self.send_sem, self.recv_sem = refs[10:]
         self.groups, self.across = self.part.shape[:2]
         self.half, self.eighth = self.groups // 2, self.groups // 8
-        self.copies = []
-
-    def send(self, src, dst, device):
-        used = len(self.copies)
-        copy = send(src, dst, self.send_sem.at[used], self.recv_sem.at[used], device)
-        self.copies.append(copy)
-        return copy
+        self.sent = []
+
+    def send(self, src, dst, to, here, device):
+        send(src, dst, self.send_sem.at[here], self.recv_sem.at[to], device)
+
+    def all_sent(self, like, here):
+        self.sent.append((like, here))
+
+    def arrived(self, like, to):
+        pltpu.make_async_copy(like, like, self.recv_sem.at[to]).wait()
 
     def start_core(self):
         p = self.place
-        self.c1 = self.send(self.part.at[pl.ds(self.half * (1 - p.core), self.half)], self.from_core, p.at(core=1))
+        self.send(self.part.at[pl.ds(self.half * (1 - p.core), self.half)], self.from_core, 0, 0, p.at(core=1))
+        self.all_sent(self.from_core, 0)
+
+    def add_core(self):
+        self.arrived(self.from_core, 0)
+        self.s1[...] = self.part[pl.ds(self.half * self.place.core, self.half)] + self.from_core[...]
 
     def start_y(self):
         p, n = self.place, self.eighth
-        self.c1.wait_recv()
-        self.s1[...] = self.part[pl.ds(self.half * p.core, self.half)] + self.from_core[...]
-        self.c2 = [self.send(self.s1.at[pl.ds(n * lax.rem(p.y + d, 4), n)], self.from_y.at[d - 1], p.at(y=d)) for d in (2, 1, 3)]
+        self.add_core()
+        for d in (2, 1, 3):
+            self.send(self.s1.at[pl.ds(n * lax.rem(p.y + d, 4), n)], self.from_y.at[d - 1], 6, 3, p.at(y=d))
+        self.all_sent(self.from_y, 3)
 
     def tile(self, y, z):
         return self.eighth * y + z // self.across, lax.rem(z, self.across)
 
     def start_plane(self):
         p = self.place
-        self.c1.wait_recv()
-        self.s1[...] = self.part[pl.ds(self.half * p.core, self.half)] + self.from_core[...]
-        self.c3 = []
+        self.add_core()
         for n, (y, z) in enumerate(PLANE):
             there = self.tile(lax.rem(p.y + y, 4), lax.rem(p.z + z, 8))
-            self.c3.append(self.send(self.s1.at[there], self.from_plane.at[n], p.at(y=y, z=z)))
+            self.send(self.s1.at[there], self.from_plane.at[n], 6, 3, p.at(y=y, z=z))
+        self.all_sent(self.from_plane, 3)
 
     def end_plane(self):
-        terms = [self.s1[self.tile(self.place.y, self.place.z)]]
-        for n in reversed(range(len(PLANE))):
-            self.c3[n].wait_recv()
-            terms.append(self.from_plane[n])
+        self.arrived(self.from_plane, 6)
+        terms = [self.s1[self.tile(self.place.y, self.place.z)]] + [self.from_plane[n] for n in range(len(PLANE))]
         while len(terms) > 1:
             terms = [a + b for a, b in zip(terms[::2], terms[1::2])]
         return terms[0]
 
     def start_z(self):
         p, n = self.place, self.eighth
-        for c in self.c2:
-            c.wait_recv()
+        self.arrived(self.from_y, 6)
         self.s2[...] = (self.s1[pl.ds(n * p.y, n)] + self.from_y[0]) + (self.from_y[1] + self.from_y[2])
-        self.c3 = []
         for d in (4, 3, 5, 2, 6, 1, 7):
             there = lax.rem(p.z + d, 8)
-            self.c3.append(self.send(self.s2.at[there // self.across, lax.rem(there, self.across)], self.from_z.at[d - 1], p.at(z=d)))
+            self.send(self.s2.at[there // self.across, lax.rem(there, self.across)], self.from_z.at[d - 1], 7, 4, p.at(z=d))
+        self.all_sent(self.from_z, 4)
 
     def end_z(self):
         p = self.place
-        for c in self.c3:
-            c.wait_recv()
+        self.arrived(self.from_z, 7)
         f = self.from_z
         total = self.s2[p.z // self.across, lax.rem(p.z, self.across)]
         return ((total + f[0]) + (f[1] + f[2])) + ((f[3] + f[4]) + (f[5] + f[6]))
@@ -109,7 +113,9 @@
     def start_x(self):
         p = self.place
         self.s3[...] = self.end_z()
-        self.c4 = [self.send(self.s3, self.from_x.at[p.x], p.at(x=d)) for d in (2, 1, 3)]
+        for d in (2, 1, 3):
+            self.send(self.s3, self.from_x.at[p.x], 8, 5, p.at(x=d))
+        self.all_sent(self.from_x.at[pl.ds(0, 3)], 5)
         self.from_x[p.x] = self.s3[...]
 
     def start_gather(self):
@@ -117,31 +123,29 @@
         group, across = self.tile(p.y, p.z)
         group = self.half * p.core + group
         if self.over_x:
-            for c in self.c4:
-                c.wait_recv()
+            self.arrived(self.from_x.at[pl.ds(0, 3)], 8)
             self.full[group, across] = (self.from_x[0] + self.from_x[1]) + (self.from_x[2] + self.from_x[3])
         else:
             self.full[group, across] = self.end_plane()
         mine = self.full.at[group, across]
-        self.c5 = [self.send(mine, mine, p.at(y=y, z=z)) for y, z in PLANE]
+        for y, z in PLANE:
+            self.send(mine, mine, 1 + y, 1, p.at(y=y, z=z))
+        self.all_sent(self.from_plane, 1)
 
     def start_gather_core(self):
         p = self.place
-        self.c7 = []
         for step in (0, 1, 3, 2):
-            for c, (y, z) in zip(self.c5, PLANE):
-                if y == (4 - step) % 4:
-                    c.wait_recv()
             rows = self.full.at[pl.ds(self.half * p.core + self.eighth * lax.rem(p.y + step, 4), self.eighth)]
-            self.c7.append(self.send(rows, rows, p.at(core=1)))
+            self.arrived(rows if step else self.from_z, 1 + (4 - step) % 4)
+            self.send(rows, rows, 5, 2, p.at(core=1))
+        self.all_sent(self.from_core, 2)
 
     def finish(self):
-        for c in self.c7:
-            c.wait_recv()
+        self.arrived(self.from_core, 5)
 
     def drain(self):
-        for c in self.copies:
-            c.wait_send()
+        for like, here in self.sent:
+            pltpu.make_async_copy(like, like, self.send_sem.at[here]).wait()
 
 
 def tiled(matrix):
@@ -262,21 +266,22 @@
     steps = (1, 3)
     x_copies = []
 
-    def side_copy(source, q, half, side, slot):
-        rows = block.at[source, q, pl.ds(256 * half, 256)]
-        at = 6 * q + 2 * slot + side
-        copy = send(rows, rows, side_send.at[at], side_recv.at[at], p.at(x=steps[side]))
+    def side_copy(source, q, start, count, side):
+        rows = block.at[source, q, pl.ds(start, count)]
+        at = len(x_copies)
+        copy = send(rows, rows, side_send.at[0], side_recv.at[at], p.at(x=steps[side]))
         x_copies.append(copy)
         return copy
 
-    def direct(q, n):
-        return [side_copy(p.x, q, n if side == 0 else 1 - n, side, n) for side in range(2)]
-
-    def relay(q, arrived):
+    def direct(q, n, start=0, count=256):
+        return [side_copy(p.x, q, 256 * (n if side == 0 else 1 - n) + start, count, side) for side in range(2)]
+
+    def relay(q, *arrived):
         copies = []
         for side in range(2):
-            arrived[side].wait_recv()
-            copies.append(side_copy(lax.rem(p.x + steps[1 - side], 4), q, side, side, 2))
+            for pair in arrived:
+                pair[side].wait_recv()
+            copies.append(side_copy(lax.rem(p.x + steps[1 - side], 4), q, 256 * side, 256, side))
         return copies
 
     def wait(copies):
@@ -295,46 +300,47 @@
     for h, tile in enumerate(tiled(dot(mine.T, mine))):
         g.part[:, h] = tile
     g.start_core()
+    g.start_y()
     load.wait()
     add_cross(0, 0, True)
-    g.start_y()
     relay0 = relay(0, first0)
-    first1 = direct(1, 0)
+    first1 = direct(1, 0, 0, 128)
+    g.start_z()
     add_cross(1, 0, True)
-    g.start_z()
     wait(second0)
     add_cross(0, 1)
     add_cross(0, 3)
     g.start_x()
+    rest1 = direct(1, 0, 128, 128)
     second1 = direct(1, 1)
     wait(relay0)
     add_cross(0, 2)
     t[0].start_core()
-    relay1 = relay(1, first1)
     t[0].start_plane()
     g.start_gather()
+    relay1 = relay(1, first1, rest1)
     wait(second1)
     add_cross(1, 1)
     add_cross(1, 3)
+    t[0].start_gather()
     wait(relay1)
     add_cross(1, 2)
     t[1].start_core()
     g.start_gather_core()
     t[1].start_plane()
-    t[0].start_gather()
     g.finish()
     a[...] = g.full[...]
     factor_part(0, a, r, inv)
     factor_part(1, a, r, inv)
     factor_part(2, a, r, inv)
-    t[1].start_gather()
     factor_part(3, a, r, inv)
     t[0].start_gather_core()
+    factor_part(4, a, r, inv)
+    t[1].start_gather()
     for x in range(4):
         for q in range(2):
             at = (pl.ds(512 * x, 512), pl.ds(128 * q, 128))
             block_high[at], block_low[at] = split(block[x, q])
-    factor_part(4, a, r, inv)
     factor_part(5, a, r, inv)
     factor_part(6, a, r, inv)
     factor_part(7, a, r, inv)
@@ -350,8 +356,8 @@
     lower = whole(t[1].full)
     weight_high[...], weight_low[...] = split(weight + dot(square[:, 128:], lower))
     projected[128:, :] = projected[128:, :] + dot(inverse[128:, 128:], lower)
-    for copy in x_copies:
-        copy.wait_send()
+    sent = block.at[pl.ds(0, 3)]
+    pltpu.make_async_copy(sent, sent, side_send.at[0]).wait()
     for reduction in (g, *t):
         reduction.drain()
 
@@ -361,7 +367,7 @@
     return [
         tiles(groups, across), tiles(groups // 2, across), tiles(groups // 2, across), tiles(3, groups // 8, across),
         tiles(groups // 8, across), tiles(7), tiles(len(PLANE)), tiles(), tiles(4), tiles(groups, across),
-        pltpu.SemaphoreType.DMA((72,)), pltpu.SemaphoreType.DMA((72,)),
+        pltpu.SemaphoreType.DMA((6,)), pltpu.SemaphoreType.DMA((9,)),
     ]
 
 
@@ -387,8 +393,8 @@
             halves,
             halves,
             pltpu.SemaphoreType.DMA((3,)),
-            pltpu.SemaphoreType.DMA((12,)),
-            pltpu.SemaphoreType.DMA((12,)),
+            pltpu.SemaphoreType.DMA((1,)),
+            pltpu.SemaphoreType.DMA((14,)),
             *scratch(32, 2),
             *scratch(16, 4),
             *scratch(16, 4),

time: 58.8 us -> 52.3 us (0.89)
  Pallas kernels: 57.9 us -> 51.4 us
    pallas_call x1, Pallas kernels: 55.2 us -> 48.7 us  [main_part(): pl.pallas_call(main_kernel, out_shape=(jax.ShapeDtypeStruct((2048, 256),...]
where the time goes in v4:
time: 52.3 us; the launch traced here: 52.2 us
  Pallas kernels  51.4 us (98%)
  between operations  0.8 us (2%)
    pallas_call x1, Pallas kernels, main_part(): pl.pallas_call(main_kernel, out_shape=(jax.ShapeDtypeStruct((2048, 256),...  48.7 us
    pallas_call x1, Pallas kernels, update(): pl.pallas_call(update_kernel, out_shape=(jax.ShapeDtypeStruct((256, 256),...  2.68 us

profile of v4, /device:TPU:1, one launch (start us, length us, event | category | flops | bytes accessed | tf_op | source)
XLA Modules:
  0.0 52.2 jit_solution(1486740212500927284)
XLA Ops:
  0.6 48.7 %shard_map.49 = (bf16[2048,256]{1,0:T(8,128)(2,1)S(1)}, bf16[2048,256]{1,0:T(8,128)(2,1)S(1)}, f32[256,256]{1,0:T(8,128)S(1)}, f32[256,512]{1,0:T(8,128)S(1)}, b...) custom-call(f32[512,256]{1,0:T(8,128)} %panel.1, f32[2048,512]{1,0:T(8,128)} %trailing.1), custom_call_target="tpu_custom_call" | custom-call | tf_op jit(solution)/shard_map/pallas_call | solution.py:377
  49.3 2.7 %shard_map.50 = (f32[256,256]{1,0:T(8,128)}, f32[256,512]{1,0:T(8,128)}, f32[2048,512]{1,0:T(8,128)}) custom-call(f32[2048,512]{1,0:T(8,128)S(1)} %get-tuple-element.10.held, bf16[2048,256]{1,0:T(8,128)(2,1)S(1)} %get-tuple-element.11.high, bf16[2048,256]{1,0:T(8,128)(2,1)S(1)} %get-tuple-element.12.low, bf16[256,512]{1,0:T(8,128)(2,1)S(1)} %get-tuple-element.13.weight_high, ...), custom_call_target="tpu_custom_call" | custom-call | tf_op jit(solution)/shard_map/pallas_call | solution.py:432

commit v5 on v4

--- a/solution.py
+++ b/solution.py
@@ -241,7 +241,7 @@
 
 def main_kernel(
     panel, trailing, block_high, block_low, rfactor, projected, weight_high, weight_low, held,
-    block, a, inv, r, load_sem, side_send, side_recv, *rest
+    block, a, inv, r, load_sem, side_send, side_recv, met, *rest
 ):
     p = Place()
     g = Reduction(p, rest[:12], True)
@@ -254,11 +254,21 @@
         own.start()
     load = pltpu.make_async_copy(trailing, held, load_sem.at[2])
 
+    beside = {axis: [p.at(**{axis: d}) for d in (1, size - 1)] for axis, size in (("y", 4), ("z", 8), ("x", 4))}
     barrier = pltpu.get_barrier_semaphore()
-    peers = [p.at(core=1)] + [p.at(y=d) for d in (1, 2, 3)] + [p.at(z=d) for d in range(1, 8)] + [p.at(x=d) for d in (1, 2, 3)]
-    for peer in peers:
+    for peer in [p.at(core=1)] + beside["y"] + beside["z"] + beside["x"]:
         pl.semaphore_signal(barrier, inc=1, device_id=peer, device_id_type=MESH)
-    pl.semaphore_wait(barrier, len(peers))
+    pl.semaphore_wait(barrier, 7)
+
+    def tell(axis, at):
+        for peer in beside[axis]:
+            pl.semaphore_signal(met.at[at], inc=1, device_id=peer, device_id_type=MESH)
+
+    def hear(at):
+        pl.semaphore_wait(met.at[at], 2)
+
+    for at, axis in enumerate(("y", "x", "z")):
+        tell(axis, at)
     for own in owns:
         own.wait()
     load.start()
@@ -300,11 +310,18 @@
     for h, tile in enumerate(tiled(dot(mine.T, mine))):
         g.part[:, h] = tile
     g.start_core()
+    hear(0)
+    hear(2)
+    tell("z", 3)
     g.start_y()
+    hear(3)
+    tell("z", 4)
     load.wait()
     add_cross(0, 0, True)
     relay0 = relay(0, first0)
     first1 = direct(1, 0, 0, 128)
+    hear(4)
+    hear(1)
     g.start_z()
     add_cross(1, 0, True)
     wait(second0)
@@ -395,6 +412,7 @@
             pltpu.SemaphoreType.DMA((3,)),
             pltpu.SemaphoreType.DMA((1,)),
             pltpu.SemaphoreType.DMA((14,)),
+            pltpu.SemaphoreType.REGULAR((5,)),
             *scratch(32, 2),
             *scratch(16, 4),
             *scratch(16, 4),

time: 52.3 us -> 50.4 us (0.964)
  Pallas kernels: 51.4 us -> 49.5 us
    pallas_call x1, Pallas kernels: 48.7 us -> 46.8 us  [main_part(): pl.pallas_call(main_kernel, out_shape=(jax.ShapeDtypeStruct((2048, 256),...]
where the time goes in v5:
time: 50.4 us; the launch traced here: 50.3 us
  Pallas kernels  49.5 us (98%)
  between operations  0.8 us (2%)
    pallas_call x1, Pallas kernels, main_part(): pl.pallas_call(main_kernel, out_shape=(jax.ShapeDtypeStruct((2048, 256),...  46.8 us
    pallas_call x1, Pallas kernels, update(): pl.pallas_call(update_kernel, out_shape=(jax.ShapeDtypeStruct((256, 256),...  2.68 us

profile of v5, /device:TPU:1, one launch (start us, length us, event | category | flops | bytes accessed | tf_op | source)
XLA Modules:
  0.0 50.3 jit_solution(7788899292930495081)
XLA Ops:
  0.6 46.8 %shard_map.49 = (bf16[2048,256]{1,0:T(8,128)(2,1)S(1)}, bf16[2048,256]{1,0:T(8,128)(2,1)S(1)}, f32[256,256]{1,0:T(8,128)S(1)}, f32[256,512]{1,0:T(8,128)S(1)}, b...) custom-call(f32[512,256]{1,0:T(8,128)} %panel.1, f32[2048,512]{1,0:T(8,128)} %trailing.1), custom_call_target="tpu_custom_call" | custom-call | tf_op jit(solution)/shard_map/pallas_call | solution.py:394
  47.4 2.7 %shard_map.50 = (f32[256,256]{1,0:T(8,128)}, f32[256,512]{1,0:T(8,128)}, f32[2048,512]{1,0:T(8,128)}) custom-call(f32[2048,512]{1,0:T(8,128)S(1)} %get-tuple-element.10.held, bf16[2048,256]{1,0:T(8,128)(2,1)S(1)} %get-tuple-element.11.high, bf16[2048,256]{1,0:T(8,128)(2,1)S(1)} %get-tuple-element.12.low, bf16[256,512]{1,0:T(8,128)(2,1)S(1)} %get-tuple-element.13.weight_high, ...), custom_call_target="tpu_custom_call" | custom-call | tf_op jit(solution)/shard_map/pallas_call | solution.py:450

commit v6 on v5

--- a/solution.py
+++ b/solution.py
@@ -60,10 +60,12 @@
     def arrived(self, like, to):
         pltpu.make_async_copy(like, like, self.recv_sem.at[to]).wait()
 
-    def start_core(self):
-        p = self.place
-        self.send(self.part.at[pl.ds(self.half * (1 - p.core), self.half)], self.from_core, 0, 0, p.at(core=1))
-        self.all_sent(self.from_core, 0)
+    def start_core(self, column=0, columns=None):
+        p, n = self.place, columns or self.across
+        theirs = self.part.at[pl.ds(self.half * (1 - p.core), self.half), pl.ds(column, n)]
+        self.send(theirs, self.from_core.at[:, pl.ds(column, n)], 0, 0, p.at(core=1))
+        if column + n == self.across:
+            self.all_sent(self.from_core, 0)
 
     def add_core(self):
         self.arrived(self.from_core, 0)
@@ -239,6 +241,13 @@
     return high, (x - high.astype(F32)).astype(jnp.bfloat16)
 
 
+def split3(x):
+    high = x.astype(jnp.bfloat16)
+    rest = x - high.astype(F32)
+    middle = rest.astype(jnp.bfloat16)
+    return high, middle, (rest - middle.astype(F32)).astype(jnp.bfloat16)
+
+
 def main_kernel(
     panel, trailing, block_high, block_low, rfactor, projected, weight_high, weight_low, held,
     block, a, inv, r, load_sem, side_send, side_recv, met, *rest
@@ -274,38 +283,31 @@
     load.start()
 
     steps = (1, 3)
-    x_copies = []
-
-    def side_copy(source, q, start, count, side):
+    def side_copy(source, q, start, count, side, to):
         rows = block.at[source, q, pl.ds(start, count)]
-        at = len(x_copies)
-        copy = send(rows, rows, side_send.at[0], side_recv.at[at], p.at(x=steps[side]))
-        x_copies.append(copy)
-        return copy
-
-    def direct(q, n, start=0, count=256):
-        return [side_copy(p.x, q, 256 * (n if side == 0 else 1 - n) + start, count, side) for side in range(2)]
-
-    def relay(q, *arrived):
-        copies = []
+        send(rows, rows, side_send.at[0], side_recv.at[to], p.at(x=steps[side]))
+
+    def direct(to, q, n, start=0, count=256):
         for side in range(2):
-            for pair in arrived:
-                pair[side].wait_recv()
-            copies.append(side_copy(lax.rem(p.x + steps[1 - side], 4), q, 256 * side, 256, side))
-        return copies
-
-    def wait(copies):
-        for copy in copies:
-            copy.wait_recv()
-
-    def add_cross(q, step, first=False):
+            side_copy(p.x, q, 256 * (n if side == 0 else 1 - n) + start, count, side, to)
+
+    def wait(at):
+        like = block.at[0, 0]
+        pltpu.make_async_copy(like, like, side_recv.at[at]).wait()
+
+    def relay(to, q, at):
+        wait(at)
+        for side in range(2):
+            side_copy(lax.rem(p.x + steps[1 - side], 4), q, 256 * side, 256, side, to)
+
+    def add_cross(q, step, first=False, columns=(0, 1, 2, 3)):
         x = lax.rem(p.x + step, 4)
-        terms = tiled(dot(block[x, q].T, held[pl.ds(512 * x, 512), :]))
-        for h in range(4):
-            t[q].part[:, h] = terms[h] if first else t[q].part[:, h] + terms[h]
-
-    first0 = direct(0, 0)
-    second0 = direct(0, 1)
+        right = held[pl.ds(512 * x, 512), 128 * columns[0] : 128 * columns[-1] + 128]
+        for h, term in zip(columns, tiled(dot(block[x, q].T, right))):
+            t[q].part[:, h] = term if first else t[q].part[:, h] + term
+
+    direct(0, 0, 0)
+    direct(1, 0, 1)
     mine = jnp.concatenate([block[p.x, q] for q in range(2)], axis=1)
     for h, tile in enumerate(tiled(dot(mine.T, mine))):
         g.part[:, h] = tile
@@ -318,31 +320,33 @@
     tell("z", 4)
     load.wait()
     add_cross(0, 0, True)
-    relay0 = relay(0, first0)
-    first1 = direct(1, 0, 0, 128)
+    relay(2, 0, 0)
+    direct(3, 1, 0, 0, 128)
     hear(4)
     hear(1)
     g.start_z()
     add_cross(1, 0, True)
-    wait(second0)
+    wait(1)
     add_cross(0, 1)
     add_cross(0, 3)
     g.start_x()
-    rest1 = direct(1, 0, 128, 128)
-    second1 = direct(1, 1)
-    wait(relay0)
+    direct(3, 1, 0, 128, 128)
+    direct(4, 1, 1)
+    wait(2)
     add_cross(0, 2)
     t[0].start_core()
     t[0].start_plane()
     g.start_gather()
-    relay1 = relay(1, first1, rest1)
-    wait(second1)
+    relay(5, 1, 3)
+    wait(4)
     add_cross(1, 1)
     add_cross(1, 3)
     t[0].start_gather()
-    wait(relay1)
-    add_cross(1, 2)
-    t[1].start_core()
+    wait(5)
+    add_cross(1, 2, False, (0, 1))
+    t[1].start_core(0, 2)
+    add_cross(1, 2, False, (2, 3))
+    t[1].start_core(2, 2)
     g.start_gather_core()
     t[1].start_plane()
     g.finish()
@@ -351,7 +355,6 @@
     factor_part(1, a, r, inv)
     factor_part(2, a, r, inv)
     factor_part(3, a, r, inv)
-    t[0].start_gather_core()
     factor_part(4, a, r, inv)
     t[1].start_gather()
     for x in range(4):
@@ -359,6 +362,7 @@
             at = (pl.ds(512 * x, 512), pl.ds(128 * q, 128))
             block_high[at], block_low[at] = split(block[x, q])
     factor_part(5, a, r, inv)
+    t[0].start_gather_core()
     factor_part(6, a, r, inv)
     factor_part(7, a, r, inv)
     rfactor[...] = whole(r)
@@ -368,23 +372,28 @@
     upper = whole(t[0].full)
     projected[...] = dot(inverse[:, :128], upper)
     weight = dot(square[:, :128], upper)
+    high, middle, low = split3(jnp.concatenate([square[:, 128:], inverse[128:, 128:]], axis=0))
+    left = jnp.concatenate([high, middle], axis=1), jnp.concatenate([high, low], axis=1)
     t[1].start_gather_core()
     t[1].finish()
-    lower = whole(t[1].full)
-    weight_high[...], weight_low[...] = split(weight + dot(square[:, 128:], lower))
-    projected[128:, :] = projected[128:, :] + dot(inverse[128:, 128:], lower)
+    high, middle, low = split3(whole(t[1].full))
+    mul = functools.partial(jnp.dot, preferred_element_type=F32)
+    twice = lambda a, b: jnp.concatenate([a, b], axis=0)
+    product = mul(left[0], twice(high, high)) + (mul(left[0], twice(middle, middle)) + mul(left[1], twice(low, high)))
+    weight_high[...], weight_low[...] = split(weight + product[:256])
+    projected[128:, :] = projected[128:, :] + product[256:]
     sent = block.at[pl.ds(0, 3)]
     pltpu.make_async_copy(sent, sent, side_send.at[0]).wait()
     for reduction in (g, *t):
         reduction.drain()
 
 
-def scratch(groups, across):
+def scratch(groups, across, sends, receives):
     tiles = lambda *shape: pltpu.VMEM((*shape, 8, 128), F32)
     return [
         tiles(groups, across), tiles(groups // 2, across), tiles(groups // 2, across), tiles(3, groups // 8, across),
         tiles(groups // 8, across), tiles(7), tiles(len(PLANE)), tiles(), tiles(4), tiles(groups, across),
-        pltpu.SemaphoreType.DMA((6,)), pltpu.SemaphoreType.DMA((9,)),
+        pltpu.SemaphoreType.DMA((sends,)), pltpu.SemaphoreType.DMA((receives,)),
     ]
 
 
@@ -411,11 +420,11 @@
             halves,
             pltpu.SemaphoreType.DMA((3,)),
             pltpu.SemaphoreType.DMA((1,)),
-            pltpu.SemaphoreType.DMA((14,)),
+            pltpu.SemaphoreType.DMA((6,)),
             pltpu.SemaphoreType.REGULAR((5,)),
-            *scratch(32, 2),
-            *scratch(16, 4),
-            *scratch(16, 4),
+            *scratch(32, 2, 6, 9),
+            *scratch(16, 4, 4, 7),
+            *scratch(16, 4, 4, 7),
         ],
         compiler_params=pltpu.CompilerParams(collective_id=0, has_side_effects=True, vmem_limit_bytes=40 << 20),
     )(panel, trailing)

time: 50.4 us -> 50.6 us (level)
  no operation moved by 1% of the time
where the time goes in v6:
time: 50.6 us; the launch traced here: 50.5 us
  Pallas kernels  49.7 us (98%)
  between operations  0.8 us (2%)
    pallas_call x1, Pallas kernels, main_part(): pl.pallas_call(main_kernel, out_shape=(jax.ShapeDtypeStruct((2048, 256),...  47 us
    pallas_call x1, Pallas kernels, update(): pl.pallas_call(update_kernel, out_shape=(jax.ShapeDtypeStruct((256, 256),...  2.68 us

profile of v6, /device:TPU:1, one launch (start us, length us, event | category | flops | bytes accessed | tf_op | source)
XLA Modules:
  0.0 50.5 jit_solution(1012684012609255914)
XLA Ops:
  0.6 47.0 %shard_map.49 = (bf16[2048,256]{1,0:T(8,128)(2,1)S(1)}, bf16[2048,256]{1,0:T(8,128)(2,1)S(1)}, f32[256,256]{1,0:T(8,128)S(1)}, f32[256,512]{1,0:T(8,128)S(1)}, b...) custom-call(f32[512,256]{1,0:T(8,128)} %panel.1, f32[2048,512]{1,0:T(8,128)} %trailing.1), custom_call_target="tpu_custom_call" | custom-call | tf_op jit(solution)/shard_map/pallas_call | solution.py:403
  47.7 2.7 %shard_map.50 = (f32[256,256]{1,0:T(8,128)}, f32[256,512]{1,0:T(8,128)}, f32[2048,512]{1,0:T(8,128)}) custom-call(f32[2048,512]{1,0:T(8,128)S(1)} %get-tuple-element.10.held, bf16[2048,256]{1,0:T(8,128)(2,1)S(1)} %get-tuple-element.11.high, bf16[2048,256]{1,0:T(8,128)(2,1)S(1)} %get-tuple-element.12.low, bf16[256,512]{1,0:T(8,128)(2,1)S(1)} %get-tuple-element.13.weight_high, ...), custom_call_target="tpu_custom_call" | custom-call | tf_op jit(solution)/shard_map/pallas_call | solution.py:459
